TPU v7x, 256 devices: a whole 4x4x8 slice. The times are simulated.
256 devices in a mesh: gx: 32 (over y, z), gy: 8 (over x, core).
Axes of the slice: x: 4, y: 4, z: 8, core: 2. Of those that a mesh axis runs over, the one named last changes fastest.
Arguments:
- loads: float32 [64, 393216], P(None, ('gx', 'gy')), may hold values from -6 to 6
- guess: float32 [64, 393216], P(None, ('gx', 'gy')), may hold values from -4 to 4
- mass: float32 [393216], P(('gx', 'gy')), may hold values from 0.5 to 4
- moduli: float32 [393216], P(('gx', 'gy')), may hold values from 0.3 to 3
- tiles: float32 [10240, 256, 256], P(('gx', 'gy')), may hold values from -0.21875 to 0.21875
- tile_row: int32 [10240], P(('gx', 'gy')), may hold values from -1 to 5, as said below
- tile_col: int32 [10240], P(('gx', 'gy')), may hold values from 0 to 21, as said below
- send_list: int32 [256, 4, 4], P(('gx', 'gy')), may hold values from -1 to 5, as said below
Outputs:
- solution: float32 [64, 393216], P(None, ('gx', 'gy'))
- residual: float32 [64, 393216], P(None, ('gx', 'gy'))
Inputs may be any that keep to these rules, and one draw needn't show every extreme that they name: `tile_row`: strain block (of the tile's own device) of each slot, -1 for an unused slot. A device's used slots come first; slot r below 6 holds the diagonal tile of block r; some device uses all 40 slots. `tile_col`: column block of each slot in its device's extended numbering: below 6 an own block; 6 + g * 4 + k the k-th entry of the list that neighbour g (0 below along gx, 1 above along gx, 2 below along gy, 3 above along gy) sends to this device. Used slots read only entries that are not -1, every such entry is read by some slot, unused slots hold 0. `send_list`: for each device and each neighbour in the order below gx, above gx, below gy, above gy: distinct own blocks to send, padded with -1 at the end; all -1 toward a missing neighbour; some lists are full.
All inputs are finite; a program needn't handle non-finite values.
Results may differ from a plain program's by a relative error of at most 0.0003.
Values sent between devices are 32-bit elements; how exact they have to be, the bound alone decides.
A program may use at most 128 MiB of HBM per device.

v0:
```python
import functools

import jax
import jax.numpy as jnp
from jax import lax
from jax.experimental import pallas as pl
from jax.experimental.pallas import tpu as pltpu
from jax.sharding import PartitionSpec as P

MESH = pl.DeviceIdType.MESH
GROUPS = 2
CHUNKS = 8
UNROLL = 20
F32 = jnp.float32
BF16 = jnp.bfloat16


class Tables:
    def __init__(self, slots, blocks, depth):
        self.slots, self.blocks, self.depth = slots, blocks, depth
        self.extent = blocks + 4 * depth
        at = 0

        def take(n):
            nonlocal at
            start = at
            at += n
            return start

        self.row_slot = take(slots)
        self.row_col = take(slots)
        self.row_keep = take(slots + 8)
        self.col_slot = take(slots)
        self.col_row = take(slots)
        self.col_keep = take(slots + 8)
        self.row_last = take(blocks + 2)
        self.col_last = take(self.extent + 2)
        self.col_has = take(self.extent + 2)
        self.pack_at = take(4 * depth)
        self.pack_has = take(4 * depth)
        self.back_at = take(4 * blocks + 8)
        self.back_has = take(4 * blocks + 8)
        self.size = -(-at // 128) * 128


def index_kernel(tb, row_ref, col_ref, list_ref, out_ref, first_ref, next_ref):
    slots, blocks, depth, extent = tb.slots, tb.blocks, tb.depth, tb.extent

    def row_key(t):
        row = row_ref[t]
        return jnp.where(row < 0, blocks, row)

    def col_key(t):
        return jnp.where(row_ref[t] < 0, extent, col_ref[t])

    def sort(key, keys, slot_at, other_at, keep_at, other):
        for k in range(keys + 1):
            next_ref[k] = 0

        def count(t, c):
            k = key(t)
            next_ref[k] = next_ref[k] + 1
            return c

        lax.fori_loop(0, slots, count, 0, unroll=True)
        at = jnp.int32(0)
        for k in range(keys + 1):
            n = next_ref[k]
            first_ref[k] = at
            next_ref[k] = at
            at = at + n

        def place(t, c):
            k = key(t)
            p = next_ref[k]
            next_ref[k] = p + 1
            out_ref[slot_at + p] = t
            out_ref[other_at + p] = other(t)
            out_ref[keep_at + p] = 1
            return c

        lax.fori_loop(0, slots, place, 0, unroll=True)
        for k in range(keys + 1):
            out_ref[keep_at + first_ref[k]] = 0

    sort(row_key, blocks, tb.row_slot, tb.row_col, tb.row_keep, lambda t: col_ref[t])
    for k in range(blocks):
        out_ref[tb.row_last + k] = jnp.maximum(next_ref[k] - 1, 0)
    sort(col_key, extent, tb.col_slot, tb.col_row, tb.col_keep, lambda t: jnp.maximum(row_ref[t], 0))
    for k in range(extent):
        out_ref[tb.col_last + k] = jnp.maximum(next_ref[k] - 1, 0)
        out_ref[tb.col_has + k] = jnp.where(next_ref[k] > first_ref[k], 1, 0)
    for k in range(4 * blocks + 8):
        out_ref[tb.back_at + k] = 0
        out_ref[tb.back_has + k] = 0
    for d in range(4):
        for h in range(depth):
            r = list_ref[0, d, h]
            has = jnp.where(r >= 0, 1, 0)
            out_ref[tb.pack_at + d * depth + h] = jnp.maximum(r, 0)
            out_ref[tb.pack_has + d * depth + h] = has
            spot = jnp.where(r >= 0, d * blocks + r, 4 * blocks)
            out_ref[tb.back_at + spot] = h
            out_ref[tb.back_has + spot] = has


def halves(value):
    high = value.astype(BF16)
    return high, (value - high.astype(F32)).astype(BF16)


def solve_kernel(
    tb, n_gx, n_gy, n_z,
    tab, mass, moduli, guess, loads, tiles,
    sol, res,
    stage, tile, tile_t, hist, ext, stress, scan, own, strain0, norm0, coef,
    send_f, recv_f, send_r, recv_r, red_send, red_recv,
    tile_sem, fs_sem, fr_sem, rs_sem, rr_sem, ds_sem, dr_sem,
):
    slots, blocks, depth = tb.slots, tb.blocks, tb.depth
    block = mass.shape[1] // blocks
    rows = hist.shape[3]
    groups = range(GROUPS)
    gx, gy = lax.axis_index("gx"), lax.axis_index("gy")
    n_y = n_gx // n_z
    y, z = gx // n_z, gx % n_z

    def chip(yy, zz):
        return yy * n_z + zz

    around = [
        ((gx + n_gx - 1) % n_gx, gy),
        ((gx + 1) % n_gx, gy),
        (gx, (gy + n_gy - 1) % n_gy),
        (gx, (gy + 1) % n_gy),
    ]
    phases = [
        [(gx, (gy + k) % n_gy) for k in range(1, n_gy)],
        [(chip((y + k) % n_y, z), gy) for k in range(1, n_y)],
        [(chip(y, (z + k) % n_z), gy) for k in range(1, n_z)],
    ]
    starts = [0, len(phases[0]), len(phases[0]) + len(phases[1])]

    per = slots // CHUNKS
    loads_in = [
        pltpu.make_async_copy(tiles.at[pl.ds(c * per, per)], stage.at[pl.ds(c * per, per)], tile_sem.at[c])
        for c in range(CHUNKS)
    ]
    for copy in loads_in:
        copy.start()

    barrier = pltpu.get_barrier_semaphore()
    greet = around[:2] + phases[0] + phases[1] + phases[2]
    for device in greet:
        pl.semaphore_signal(barrier, inc=1, device_id=device, device_id_type=MESH)

    def flag(at):
        return tab[at].astype(F32)

    def lanes(ref, b):
        return ref[:, b * block : (b + 1) * block]

    def forward(g, d):
        return pltpu.make_async_remote_copy(
            src_ref=send_f.at[g, d],
            dst_ref=recv_f.at[g, d ^ 1],
            send_sem=fs_sem.at[g, d],
            recv_sem=fr_sem.at[g, d ^ 1],
            device_id=around[d],
            device_id_type=MESH,
        )

    def backward(g, d):
        return pltpu.make_async_remote_copy(
            src_ref=send_r.at[g, d],
            dst_ref=recv_r[g].at[d ^ 1],
            send_sem=rs_sem.at[g, d],
            recv_sem=rr_sem.at[g, d ^ 1],
            device_id=around[d],
            device_id_type=MESH,
        )

    def wait_recv(make, g):
        for d in range(4):
            make(g, d ^ 1).wait_recv()

    def pack(step, g):
        for d in range(4):
            for h in range(depth):
                k = d * depth + h
                send_f[g, d, h] = hist[step, g, tab[tb.pack_at + k]] * flag(tb.pack_has + k)

    def split_own(step, g):
        for b in range(blocks):
            high, low = halves(hist[step, g, b])
            ext[g, b, :rows] = high
            ext[g, b, rows:] = low

    def split_halo(g):
        for d in range(4):
            for h in range(depth):
                high, low = halves(recv_f[g, d, h])
                ext[g, blocks + d * depth + h, :rows] = high
                ext[g, blocks + d * depth + h, rows:] = low

    def sweep(source, g, weights, slot_at, block_at, keep_at):
        def body(i, total):
            for u in range(UNROLL):
                t = i * UNROLL + u
                x = source[g, tab[block_at + t]]
                both = jnp.dot(
                    jnp.concatenate([x, x], axis=1), weights[tab[slot_at + t]], preferred_element_type=F32
                )
                total = total * flag(keep_at + t) + (both[:rows] + both[rows:])
                scan[t] = total
            return total

        lax.fori_loop(0, slots // UNROLL, body, jnp.zeros((rows, block), F32))

    def strain_pass(step, g):
        sweep(ext, g, tile_t, tb.row_slot, tb.row_col, tb.row_keep)
        square = jnp.zeros((rows, block), F32)
        energy = jnp.zeros((rows, block), F32)
        if step == 2:
            alpha = jnp.concatenate([coef[g, 0], coef[g, 0]], axis=1)
        for b in range(blocks):
            strain = scan[tab[tb.row_last + b]]
            module = lanes(moduli, b)
            value = module * strain
            high, low = halves(value)
            stress[g, b, :rows] = high
            stress[g, b, rows:] = low
            if step == 1:
                strain0[g, b] = strain
                r = hist[1, g, b]
                square += r * r
                energy += value * strain + lanes(mass, b) * (r * r)
            if step == 2:
                r = hist[1, g, b] - alpha * hist[2, g, b]
                mixed = strain0[g, b] - alpha * strain
                square += r * r
                energy += module * (mixed * mixed) + lanes(mass, b) * (r * r)
        return square, energy

    def back_pass(step, g):
        sweep(stress, g, tile, tb.col_slot, tb.col_row, tb.col_keep)
        if step > 0:
            for d in range(4):
                backward(g, d).wait_send()
        for d in range(4):
            for h in range(depth):
                e = blocks + d * depth + h
                send_r[g, d, h] = scan[tab[tb.col_last + e]] * flag(tb.col_has + e)
        for d in range(4):
            backward(g, d).start()
        for b in range(blocks):
            own[g, b] = scan[tab[tb.col_last + b]] * flag(tb.col_has + b) + lanes(mass, b) * hist[step, g, b]

    def total_of(g, b):
        total = own[g, b]
        for d in range(4):
            k = d * blocks + b
            total += recv_r[g][d, tab[tb.back_at + k]] * flag(tb.back_has + k)
        return total

    def reduce_copies(which, g, phase):
        return [
            pltpu.make_async_remote_copy(
                src_ref=red_send.at[which, g, phase],
                dst_ref=red_recv.at[which, g, starts[phase] + i],
                send_sem=ds_sem.at[which, g, starts[phase] + i],
                recv_sem=dr_sem.at[which, g, starts[phase] + i],
                device_id=device,
                device_id_type=MESH,
            )
            for i, device in enumerate(phases[phase])
        ]

    def reduce_start(which, g, square, energy):
        half = block // 2
        stacked = jnp.concatenate(
            [
                square[:, :half] + square[:, half:],
                energy[:, :half] + energy[:, half:],
                jnp.zeros((128 - 2 * rows, half), F32),
            ],
            axis=0,
        )
        red_send[which, g, 0] = jnp.sum(stacked.T, axis=0, keepdims=True)
        for copy in reduce_copies(which, g, 0):
            copy.start()

    def reduced(which, g, phase):
        value = red_send[which, g, phase]
        for i, copy in enumerate(reduce_copies(which, g, phase)):
            copy.wait_recv()
            value += red_recv[which, g, starts[phase] + i]
        return value

    def reduce_next(which, g, phase):
        red_send[which, g, phase + 1] = reduced(which, g, phase)
        for copy in reduce_copies(which, g, phase + 1):
            copy.start()

    def reduce_end(which, g):
        spread = jnp.broadcast_to(reduced(which, g, 2), (128, 128)).T
        return spread[:rows], spread[rows : 2 * rows]

    def wide(value):
        return jnp.concatenate([value, value], axis=1)

    for g in groups:
        for b in range(blocks):
            hist[0, g, b] = guess[g * rows : (g + 1) * rows, b * block : (b + 1) * block]
        pack(0, g)
    pl.semaphore_wait(barrier, len(greet))
    for g in groups:
        for d in range(4):
            forward(g, d).start()
        split_own(0, g)

    for c in range(CHUNKS):
        loads_in[c].wait()

        def split_tile(i, carry):
            t = c * per + i
            value = stage[t]
            high, low = halves(value)
            tile[t, :block] = high
            tile[t, block:] = low
            high, low = halves(value.T)
            tile_t[t, :block] = high
            tile_t[t, block:] = low
            return carry

        lax.fori_loop(0, per, split_tile, 0)

    def finish(step, g):
        wait_recv(backward, g)
        for b in range(blocks):
            value = total_of(g, b)
            if step == 0:
                value = loads[g * rows : (g + 1) * rows, b * block : (b + 1) * block] - value
            hist[step + 1, g, b] = value
        for d in range(4):
            forward(g, d).wait_send()
        pack(step + 1, g)
        for d in range(4):
            forward(g, d).start()
        split_own(step + 1, g)

    for step in range(2):
        for g in groups:
            wait_recv(forward, g)
            split_halo(g)
            square, energy = strain_pass(step, g)
            if step == 1:
                reduce_start(0, g, square, energy)
            back_pass(step, g)
        for g in groups:
            finish(step, g)
            if step == 1 and g == 0:
                for k in groups:
                    reduce_next(0, k, 0)
    for g in groups:
        reduce_next(0, g, 1)

    for g in groups:
        wait_recv(forward, g)
        split_halo(g)
        norm, curve = reduce_end(0, g)
        norm0[g] = norm
        coef[g, 0] = norm / curve
        square, energy = strain_pass(2, g)
        reduce_start(1, g, square, energy)
        back_pass(2, g)
    for g in groups:
        reduce_next(1, g, 0)
    for g in groups:
        reduce_next(1, g, 1)
    for g in groups:
        wait_recv(backward, g)
        norm, curve = reduce_end(1, g)
        alpha0 = coef[g, 0]
        beta = norm / norm0[g]
        alpha1 = norm / (curve - beta * norm / alpha0)
        alpha0, alpha1, beta = wide(alpha0), wide(alpha1), wide(beta)
        for b in range(blocks):
            r0, w1 = hist[1, g, b], hist[2, g, b]
            w2 = total_of(g, b)
            r1 = r0 - alpha0 * w1
            part = (slice(g * rows, (g + 1) * rows), slice(b * block, (b + 1) * block))
            sol[part] = hist[0, g, b] + alpha0 * r0 + alpha1 * (r1 + beta * r0)
            res[part] = r1 - alpha1 * (w1 - alpha0 * w2 + beta * w1)
    for g in groups:
        for d in range(4):
            forward(g, d).wait_send()
            backward(g, d).wait_send()
        for which in range(2):
            for phase in range(3):
                for copy in reduce_copies(which, g, phase):
                    copy.wait_send()


def solution(mesh):
    n_gx, n_gy = mesh.shape["gx"], mesh.shape["gy"]
    n_z = 8 if n_gx % 8 == 0 and n_gx > 8 else 2

    def on_device(loads, guess, mass, moduli, tiles, tile_row, tile_col, send_list):
        cases, width = loads.shape
        slots, block = tiles.shape[0], tiles.shape[1]
        depth = send_list.shape[2]
        blocks = width // block
        rows = cases // GROUPS
        tb = Tables(slots, blocks, depth)
        smem = pl.BlockSpec(memory_space=pltpu.SMEM)
        vmem = pl.BlockSpec(memory_space=pltpu.VMEM)
        table = pl.pallas_call(
            functools.partial(index_kernel, tb),
            out_shape=jax.ShapeDtypeStruct((tb.size,), jnp.int32),
            in_specs=[smem] * 3,
            out_specs=smem,
            scratch_shapes=[pltpu.SMEM((32,), jnp.int32), pltpu.SMEM((32,), jnp.int32)],
            name="index_tables",
        )(tile_row, tile_col, send_list)
        peers = (n_gy - 1) + (n_gx // n_z - 1) + (n_z - 1)
        halo = (GROUPS, 4, depth, rows, block)
        dma = pltpu.SemaphoreType.DMA
        return pl.pallas_call(
            functools.partial(solve_kernel, tb, n_gx, n_gy, n_z),
            out_shape=[jax.ShapeDtypeStruct((cases, width), F32)] * 2,
            in_specs=[smem, vmem, vmem, vmem, vmem, pl.BlockSpec(memory_space=pl.ANY)],
            out_specs=[vmem, vmem],
            scratch_shapes=[
                pltpu.VMEM((slots, block, block), F32),
                pltpu.VMEM((slots, 2 * block, block), BF16),
                pltpu.VMEM((slots, 2 * block, block), BF16),
                pltpu.VMEM((3, GROUPS, blocks, rows, block), F32),
                pltpu.VMEM((GROUPS, tb.extent, 2 * rows, block), BF16),
                pltpu.VMEM((GROUPS, blocks, 2 * rows, block), BF16),
                pltpu.VMEM((slots, rows, block), F32),
                pltpu.VMEM((GROUPS, blocks, rows, block), F32),
                pltpu.VMEM((GROUPS, blocks, rows, block), F32),
                pltpu.VMEM((GROUPS, rows, 128), F32),
                pltpu.VMEM((GROUPS, 1, rows, 128), F32),
                pltpu.VMEM(halo, F32),
                pltpu.VMEM(halo, F32),
                pltpu.VMEM(halo, F32),
                [pltpu.VMEM(halo[1:], F32)] * GROUPS,
                pltpu.VMEM((2, GROUPS, 3, 1, 128), F32),
                pltpu.VMEM((2, GROUPS, peers, 1, 128), F32),
                dma((CHUNKS,)),
                dma((GROUPS, 4)),
                dma((GROUPS, 4)),
                dma((GROUPS, 4)),
                dma((GROUPS, 4)),
                dma((2, GROUPS, peers)),
                dma((2, GROUPS, peers)),
            ],
            compiler_params=pltpu.CompilerParams(
                collective_id=0, has_side_effects=True, vmem_limit_bytes=60 * 1024 * 1024
            ),
            name="solve",
        )(table, mass.reshape(1, width), moduli.reshape(1, width), guess, loads, tiles)

    both = ("gx", "gy")
    return jax.shard_map(
        on_device,
        mesh=mesh,
        in_specs=(
            P(None, both), P(None, both), P(both), P(both), P(both, None, None), P(both), P(both), P(both, None, None),
        ),
        out_specs=(P(None, both), P(None, both)),
        check_vma=False,
    )
```

profile of v0, /device:TPU:32, one launch (start us, length us, event | category | flops | bytes accessed | tf_op | source)
XLA Modules:
  0.0 83.8 jit_solution(8628109779821406341)
XLA Ops:
  0.6 2.3 %index_tables.1.tab = s32[512]{0:T(512)} custom-call(s32[40]{0:T(128)} %row_ref.1, s32[40]{0:T(128)} %col_ref.1, s32[1,4,4]{2,1,0:T(4,128)} %list_ref.1), custom_call_target="tpu_custom_call" | custom-call | tf_op jit(solution)/shard_map/index_tables/pallas_call | solution.py:418
  2.9 1.3 %reshape.10.mass = f32[1,1536]{1,0:T(1,128)} reshape(f32[1536]{0:T(1024)} %param.10) | data formatting | bytes 12288 | tf_op jit(solution)/shard_map/reshape | solution.py:464
  4.2 1.3 %reshape.11.moduli = f32[1,1536]{1,0:T(1,128)} reshape(f32[1536]{0:T(1024)} %param.11) | data formatting | bytes 12288 | tf_op jit(solution)/shard_map/reshape | solution.py:464
  5.5 74.7 %solve.1 = (f32[64,1536]{1,0:T(8,128)}, f32[64,1536]{1,0:T(8,128)}) custom-call(s32[512]{0:T(512)} %index_tables.1.tab, f32[1,1536]{1,0:T(1,128)} %reshape.10.mass, f32[1,1536]{1,0:T(1,128)} %reshape.11.moduli, f32[64,1536]{1,0:T(8,128)} %guess.1, f32[64,1536]{1,0:T(8,128)} %loads.1, f32[40,256,256]{2,1,0:T(8,128)} %tiles.1), custom_call_target="tpu_custom_call" | custom-call | tf_op jit(solution)/shard_map/solve/pallas_call | solution.py:429
  80.2 1.8 %copy.12 = f32[64,1536]{1,0:T(8,128)} copy(f32[64,1536]{1,0:T(8,128)} %get-tuple-element.4) | data formatting | bytes 786432
  82.0 1.8 %copy.13 = f32[64,1536]{1,0:T(8,128)} copy(f32[64,1536]{1,0:T(8,128)} %get-tuple-element.5) | data formatting | bytes 786432
where the time goes:
time: 84.5 us; the launch traced here: 83.8 us
  Pallas kernels  77 us (91%)
  local copies, waits for them, and re-layouts  6.13 us (7%)
    pallas_call x1, Pallas kernels, on_device(): pl.pallas_call(functools.partial(solve_kernel, tb, n_gx, n_gy, n_z), out_...  74.7 us
    unnamed x2, local copies, waits for them, and re-layouts  3.54 us
    pallas_call x1, Pallas kernels, on_device(): pl.pallas_call(functools.partial(index_kernel, tb), out_shape=jax.ShapeDt...  2.31 us

commit v1 on v0

v1 whole, which is shorter than its diff:
```python
import functools

import jax
import jax.numpy as jnp
from jax import lax
from jax.experimental import pallas as pl
from jax.experimental.pallas import tpu as pltpu
from jax.sharding import PartitionSpec as P

MESH = pl.DeviceIdType.MESH
GROUPS = 2
CHUNKS = 8
UNROLL = 20
F32 = jnp.float32
BF16 = jnp.bfloat16


ROW_SLOT, ROW_COL, ROW_KEEP, COL_SLOT, COL_ROW, COL_KEEP, ROW_LAST, COL_LAST, COL_HAS = range(9)


def sorted_slots(key_of, other, lane):
    code = (key_of * 64 + other) * 64 + lane
    across = jnp.broadcast_to(code, (128, 128))
    down = across.T
    place = jnp.sum((down < across).astype(jnp.int32), axis=0, keepdims=True)
    place = jnp.broadcast_to(place, (128, 128)).T
    spot = jnp.broadcast_to(lane, (128, 128))
    here = jnp.sum(jnp.where(place == spot, down, 0), axis=0, keepdims=True)
    before = jnp.sum(jnp.where(place == spot - 1, down, 0), axis=0, keepdims=True)
    before = jnp.where(lane == 0, -1, before // 4096)
    key = down // 4096
    last = jnp.sum((key <= spot).astype(jnp.int32), axis=0, keepdims=True) - 1
    has = jnp.sum((key == spot).astype(jnp.int32), axis=0, keepdims=True)
    keep = (here // 4096 == before).astype(jnp.int32)
    return here % 64, here // 64 % 64, keep, jnp.maximum(last, 0), jnp.minimum(has, 1)


def halves(value):
    high = value.astype(BF16)
    return high, (value - high.astype(F32)).astype(BF16)


def solve_kernel(
    depth, n_gx, n_gy, n_z,
    row_ref, col_ref, send_list, mass, moduli, guess, loads, tiles,
    sol, res,
    stage, tile, tile_t, hist, rhs, ext, stress, scan, own, strain0, norm0, coef,
    send_f, recv_f, send_r, recv_r, red_send, red_recv, table, tab, back_at, back_has,
    tile_sem, in_sem, tab_sem, fs_sem, fr_sem, rs_sem, rr_sem, ds_sem, dr_sem,
):
    slots, block = stage.shape[:2]
    blocks, rows = hist.shape[2:4]
    extent = blocks + 4 * depth
    groups = range(GROUPS)
    gx, gy = lax.axis_index("gx"), lax.axis_index("gy")
    n_y = n_gx // n_z
    y, z = gx // n_z, gx % n_z

    def chip(yy, zz):
        return yy * n_z + zz

    around = [
        ((gx + n_gx - 1) % n_gx, gy),
        ((gx + 1) % n_gx, gy),
        (gx, (gy + n_gy - 1) % n_gy),
        (gx, (gy + 1) % n_gy),
    ]
    phases = [
        [(gx, (gy + k) % n_gy) for k in range(1, n_gy)],
        [(chip((y + k) % n_y, z), gy) for k in range(1, n_y)],
        [(chip(y, (z + k) % n_z), gy) for k in range(1, n_z)],
    ]
    starts = [0, len(phases[0]), len(phases[0]) + len(phases[1])]

    barrier = pltpu.get_barrier_semaphore()
    greet = around[:2] + phases[0] + phases[1] + phases[2]
    for device in greet:
        pl.semaphore_signal(barrier, inc=1, device_id=device, device_id_type=MESH)

    def piece(whole, at, g, b, n):
        return pltpu.make_async_copy(
            whole.at[pl.ds(g * rows, rows), pl.ds(b * block, block)], at.at[g, b], in_sem.at[n, g, b]
        )

    for g in groups:
        for b in range(blocks):
            piece(guess, hist.at[0], g, b, 0).start()
    per = slots // CHUNKS
    loads_in = [
        pltpu.make_async_copy(tiles.at[pl.ds(c * per, per)], stage.at[pl.ds(c * per, per)], tile_sem.at[c])
        for c in range(CHUNKS)
    ]
    for copy in loads_in:
        copy.start()
    for g in groups:
        for b in range(blocks):
            piece(loads, rhs, g, b, 1).start()

    lane = lax.broadcasted_iota(jnp.int32, (1, 128), 1)
    row_of = jnp.full((1, 128), -2, jnp.int32)
    col_of = jnp.zeros((1, 128), jnp.int32)
    for t in range(slots):
        row_of = jnp.where(lane == t, row_ref[t], row_of)
        col_of = jnp.where(lane == t, col_ref[t], col_of)
    used, spare = row_of >= 0, (row_of < -1).astype(jnp.int32)
    by_row = sorted_slots(jnp.where(used, row_of, blocks + spare), col_of, lane)
    by_col = sorted_slots(jnp.where(used, col_of, extent + spare), jnp.maximum(row_of, 0), lane)
    for at, value in enumerate(by_row[:3] + by_col[:3] + (by_row[3],) + by_col[3:]):
        table[at : at + 1] = value
    for d in range(4):
        for b in range(blocks):
            at, has = jnp.int32(0), jnp.int32(0)
            for h in range(depth):
                same = send_list[0, d, h] == b
                at, has = jnp.where(same, h, at), jnp.where(same, 1, has)
            back_at[d * blocks + b] = at
            back_has[d * blocks + b] = has

    def listed(d, h):
        entry = send_list[0, d, h]
        return jnp.maximum(entry, 0), jnp.where(entry >= 0, 1.0, 0.0)

    def flag(at, t):
        return tab[at, t].astype(F32)

    def lanes(ref, b):
        return ref[b * block : (b + 1) * block].reshape(1, block)

    def forward(g, d):
        return pltpu.make_async_remote_copy(
            src_ref=send_f.at[g, d],
            dst_ref=recv_f.at[g, d ^ 1],
            send_sem=fs_sem.at[g, d],
            recv_sem=fr_sem.at[g, d ^ 1],
            device_id=around[d],
            device_id_type=MESH,
        )

    def backward(g, d):
        return pltpu.make_async_remote_copy(
            src_ref=send_r.at[g, d],
            dst_ref=recv_r[g].at[d ^ 1],
            send_sem=rs_sem.at[g, d],
            recv_sem=rr_sem.at[g, d ^ 1],
            device_id=around[d],
            device_id_type=MESH,
        )

    def wait_recv(make, g):
        for d in range(4):
            make(g, d ^ 1).wait_recv()

    def pack(step, g):
        for d in range(4):
            for h in range(depth):
                at, has = listed(d, h)
                send_f[g, d, h] = hist[step, g, at] * has

    def split_own(step, g):
        for b in range(blocks):
            high, low = halves(hist[step, g, b])
            ext[g, b, :rows] = high
            ext[g, b, rows:] = low

    def split_halo(g):
        for d in range(4):
            for h in range(depth):
                high, low = halves(recv_f[g, d, h])
                ext[g, blocks + d * depth + h, :rows] = high
                ext[g, blocks + d * depth + h, rows:] = low

    def sweep(source, g, weights, slot_at, block_at, keep_at):
        def body(i, total):
            for u in range(UNROLL):
                t = i * UNROLL + u
                x = source[g, tab[block_at, t]]
                both = jnp.dot(
                    jnp.concatenate([x, x], axis=1), weights[tab[slot_at, t]], preferred_element_type=F32
                )
                total = total * flag(keep_at, t) + (both[:rows] + both[rows:])
                scan[t] = total
            return total

        lax.fori_loop(0, slots // UNROLL, body, jnp.zeros((rows, block), F32))

    def strain_pass(step, g):
        sweep(ext, g, tile_t, ROW_SLOT, ROW_COL, ROW_KEEP)
        square = jnp.zeros((rows, block), F32)
        energy = jnp.zeros((rows, block), F32)
        if step == 2:
            norm, curve = reduce_end(0, g)
            norm0[g] = norm
            coef[g, 0] = norm / curve
            alpha = wide(norm / curve)
        for b in range(blocks):
            strain = scan[tab[ROW_LAST, b]]
            module = lanes(moduli, b)
            value = module * strain
            high, low = halves(value)
            stress[g, b, :rows] = high
            stress[g, b, rows:] = low
            if step == 1:
                strain0[g, b] = strain
                r = hist[1, g, b]
                square += r * r
                energy += value * strain + lanes(mass, b) * (r * r)
            if step == 2:
                r = hist[1, g, b] - alpha * hist[2, g, b]
                mixed = strain0[g, b] - alpha * strain
                square += r * r
                energy += module * (mixed * mixed) + lanes(mass, b) * (r * r)
        return square, energy

    def back_pass(step, g):
        sweep(stress, g, tile, COL_SLOT, COL_ROW, COL_KEEP)
        if step > 0:
            for d in range(4):
                backward(g, d).wait_send()
        for d in range(4):
            for h in range(depth):
                e = blocks + d * depth + h
                send_r[g, d, h] = scan[tab[COL_LAST, e]] * flag(COL_HAS, e)
        for d in range(4):
            backward(g, d).start()
        for b in range(blocks):
            own[g, b] = scan[tab[COL_LAST, b]] * flag(COL_HAS, b) + lanes(mass, b) * hist[step, g, b]

    def total_of(g, b):
        total = own[g, b]
        for d in range(4):
            k = d * blocks + b
            total += recv_r[g][d, back_at[k]] * back_has[k].astype(F32)
        return total

    def reduce_copies(which, g, phase):
        return [
            pltpu.make_async_remote_copy(
                src_ref=red_send.at[which, g, phase],
                dst_ref=red_recv.at[which, g, starts[phase] + i],
                send_sem=ds_sem.at[which, g, starts[phase] + i],
                recv_sem=dr_sem.at[which, g, starts[phase] + i],
                device_id=device,
                device_id_type=MESH,
            )
            for i, device in enumerate(phases[phase])
        ]

    def reduce_start(which, g, square, energy):
        half = block // 2
        stacked = jnp.concatenate(
            [
                square[:, :half] + square[:, half:],
                energy[:, :half] + energy[:, half:],
                jnp.zeros((128 - 2 * rows, half), F32),
            ],
            axis=0,
        )
        red_send[which, g, 0] = jnp.sum(stacked.T, axis=0, keepdims=True)
        for copy in reduce_copies(which, g, 0):
            copy.start()

    def reduced(which, g, phase):
        value = red_send[which, g, phase]
        for i, copy in enumerate(reduce_copies(which, g, phase)):
            copy.wait_recv()
            value += red_recv[which, g, starts[phase] + i]
        return value

    def reduce_next(which, g, phase):
        red_send[which, g, phase + 1] = reduced(which, g, phase)
        for copy in reduce_copies(which, g, phase + 1):
            copy.start()

    def reduce_end(which, g):
        spread = jnp.broadcast_to(reduced(which, g, 2), (128, 128)).T
        return spread[:rows], spread[rows : 2 * rows]

    def wide(value):
        return jnp.concatenate([value, value], axis=1)

    for g in groups:
        for b in range(blocks):
            piece(guess, hist.at[0], g, b, 0).wait()
    for g in groups:
        pack(0, g)
    pl.semaphore_wait(barrier, len(greet))
    for g in groups:
        for d in range(4):
            forward(g, d).start()
        split_own(0, g)
    to_smem = pltpu.make_async_copy(table, tab, tab_sem)
    to_smem.start()

    for c in range(CHUNKS):
        loads_in[c].wait()

        def split_tile(i, carry):
            t = c * per + i
            value = stage[t]
            high, low = halves(value)
            tile[t, :block] = high
            tile[t, block:] = low
            high, low = halves(value.T)
            tile_t[t, :block] = high
            tile_t[t, block:] = low
            return carry

        lax.fori_loop(0, per, split_tile, 0)

    def strain_half(step, g):
        wait_recv(forward, g)
        split_halo(g)
        square, energy = strain_pass(step, g)
        if step > 0:
            reduce_start(step - 1, g, square, energy)

    def finish(step, g):
        wait_recv(backward, g)
        for b in range(blocks):
            value = total_of(g, b)
            if step == 0:
                value = rhs[g, b] - value
            hist[step + 1, g, b] = value
        for d in range(4):
            forward(g, d).wait_send()
        pack(step + 1, g)
        for d in range(4):
            forward(g, d).start()
        split_own(step + 1, g)

    def last(g):
        wait_recv(backward, g)
        norm, curve = reduce_end(1, g)
        alpha0 = coef[g, 0]
        beta = norm / norm0[g]
        alpha1 = norm / (curve - beta * norm / alpha0)
        alpha0, alpha1, beta = wide(alpha0), wide(alpha1), wide(beta)
        for b in range(blocks):
            r0, w1 = hist[1, g, b], hist[2, g, b]
            w2 = total_of(g, b)
            r1 = r0 - alpha0 * w1
            part = (slice(g * rows, (g + 1) * rows), slice(b * block, (b + 1) * block))
            sol[part] = hist[0, g, b] + alpha0 * r0 + alpha1 * (r1 + beta * r0)
            res[part] = r1 - alpha1 * (w1 - alpha0 * w2 + beta * w1)

    to_smem.wait()
    for g in groups:
        for b in range(blocks):
            piece(loads, rhs, g, b, 1).wait()

    strain_half(0, 0)
    back_pass(0, 0)
    strain_half(0, 1)
    finish(0, 0)
    back_pass(0, 1)
    strain_half(1, 0)
    finish(0, 1)
    back_pass(1, 0)
    reduce_next(0, 0, 0)
    strain_half(1, 1)
    finish(1, 0)
    reduce_next(0, 0, 1)
    back_pass(1, 1)
    reduce_next(0, 1, 0)
    strain_half(2, 0)
    finish(1, 1)
    reduce_next(0, 1, 1)
    back_pass(2, 0)
    reduce_next(1, 0, 0)
    strain_half(2, 1)
    reduce_next(1, 0, 1)
    back_pass(2, 1)
    reduce_next(1, 1, 0)
    last(0)
    reduce_next(1, 1, 1)
    last(1)
    for g in groups:
        for d in range(4):
            forward(g, d).wait_send()
            backward(g, d).wait_send()
        for which in range(2):
            for phase in range(3):
                for copy in reduce_copies(which, g, phase):
                    copy.wait_send()


def solution(mesh):
    n_gx, n_gy = mesh.shape["gx"], mesh.shape["gy"]
    n_z = 8 if n_gx % 8 == 0 and n_gx > 8 else 2

    def on_device(loads, guess, mass, moduli, tiles, tile_row, tile_col, send_list):
        cases, width = loads.shape
        slots, block = tiles.shape[0], tiles.shape[1]
        depth = send_list.shape[2]
        blocks = width // block
        rows = cases // GROUPS
        extent = blocks + 4 * depth
        smem = pl.BlockSpec(memory_space=pltpu.SMEM)
        vmem = pl.BlockSpec(memory_space=pltpu.VMEM)
        hbm = pl.BlockSpec(memory_space=pl.ANY)
        peers = (n_gy - 1) + (n_gx // n_z - 1) + (n_z - 1)
        halo = (GROUPS, 4, depth, rows, block)
        dma = pltpu.SemaphoreType.DMA
        return pl.pallas_call(
            functools.partial(solve_kernel, depth, n_gx, n_gy, n_z),
            out_shape=[pltpu.VMEM((cases, width), F32)] * 2,
            in_specs=[smem, smem, smem, vmem, vmem, hbm, hbm, hbm],
            out_specs=[vmem, vmem],
            scratch_shapes=[
                pltpu.VMEM((slots, block, block), F32),
                pltpu.VMEM((slots, 2 * block, block), BF16),
                pltpu.VMEM((slots, 2 * block, block), BF16),
                pltpu.VMEM((3, GROUPS, blocks, rows, block), F32),
                pltpu.VMEM((GROUPS, blocks, rows, block), F32),
                pltpu.VMEM((GROUPS, extent, 2 * rows, block), BF16),
                pltpu.VMEM((GROUPS, blocks, 2 * rows, block), BF16),
                pltpu.VMEM((slots, rows, block), F32),
                pltpu.VMEM((GROUPS, blocks, rows, block), F32),
                pltpu.VMEM((GROUPS, blocks, rows, block), F32),
                pltpu.VMEM((GROUPS, rows, 128), F32),
                pltpu.VMEM((GROUPS, 1, rows, 128), F32),
                pltpu.VMEM(halo, F32),
                pltpu.VMEM(halo, F32),
                pltpu.VMEM(halo, F32),
                [pltpu.VMEM(halo[1:], F32)] * GROUPS,
                pltpu.VMEM((2, GROUPS, 3, 1, 128), F32),
                pltpu.VMEM((2, GROUPS, peers, 1, 128), F32),
                pltpu.VMEM((16, 128), jnp.int32),
                pltpu.SMEM((16, 128), jnp.int32),
                pltpu.SMEM((4 * blocks,), jnp.int32),
                pltpu.SMEM((4 * blocks,), jnp.int32),
                dma((CHUNKS,)),
                dma((2, GROUPS, blocks)),
                dma,
                dma((GROUPS, 4)),
                dma((GROUPS, 4)),
                dma((GROUPS, 4)),
                dma((GROUPS, 4)),
                dma((2, GROUPS, peers)),
                dma((2, GROUPS, peers)),
            ],
            compiler_params=pltpu.CompilerParams(
                collective_id=0, has_side_effects=True, vmem_limit_bytes=60 * 1024 * 1024
            ),
            name="solve",
        )(tile_row, tile_col, send_list, mass, moduli, guess, loads, tiles)

    both = ("gx", "gy")
    return jax.shard_map(
        on_device,
        mesh=mesh,
        in_specs=(
            P(None, both), P(None, both), P(both), P(both), P(both, None, None), P(both), P(both), P(both, None, None),
        ),
        out_specs=(P(None, both), P(None, both)),
        check_vma=False,
    )
```

time: 84.5 us -> 75.8 us (0.90)
  local copies, waits for them, and re-layouts: 6.13 us -> 1.49 us
  Pallas kernels: 77 us -> 73.6 us
    pallas_call x2 -> x1, Pallas kernels: 77 us -> 73.6 us  [on_device(): pl.pallas_call(functools.partial(solve_kernel, depth, n_gx, n_gy, n_z), o...]
    reshape x2 -> x0, local copies, waits for them, and re-layouts: 2.59 us -> none  [the longest x1 1.3 us: on_device(): mass.reshape(1, width)]
    unnamed x2, local copies, waits for them, and re-layouts: 3.54 us -> 1.49 us
where the time goes in v1:
time: 75.8 us; the launch traced here: 75.7 us
  Pallas kernels  73.6 us (97%)
  local copies, waits for them, and re-layouts  1.49 us (2%)
    pallas_call x1, Pallas kernels, on_device(): pl.pallas_call(functools.partial(solve_kernel, depth, n_gx, n_gy, n_z), o...  73.6 us

profile of v1, /device:TPU:32, one launch (start us, length us, event | category | flops | bytes accessed | tf_op | source)
XLA Modules:
  0.0 75.7 jit_solution(5549385033529501806)
XLA Ops:
  0.6 73.6 %solve.1 = (f32[64,1536]{1,0:T(8,128)S(1)}, f32[64,1536]{1,0:T(8,128)S(1)}) custom-call(s32[40]{0:T(128)} %row_ref.1, s32[40]{0:T(128)} %col_ref.1, s32[1,4,4]{2,1,0:T(4,128)} %send_list.1, f32[1536]{0:T(1024)} %mass.1, f32[1536]{0:T(1024)} %moduli.1, f32[64,1536]{1,0:T(8,128)} %guess.1, f32[64,1536]{1,0:T(8,128)} %loads.1, f32[40,256,256]{2,1,0:T(8,128)} %tiles.1), custom_call_target="tpu_custom_call" | custom-call | tf_op jit(solution)/shard_map/solve/pallas_call | solution.py:404
  74.2 0.7 copy.12
  74.9 0.7 copy.13

commit v2 on v1

--- a/solution.py
+++ b/solution.py
@@ -8,11 +8,19 @@
 from jax.sharding import PartitionSpec as P
 
 MESH = pl.DeviceIdType.MESH
-GROUPS = 2
+GROUPS = 4
+LAG = 2
 CHUNKS = 8
 UNROLL = 20
 F32 = jnp.float32
 BF16 = jnp.bfloat16
+F8 = jnp.float8_e4m3fn
+LOW_SCALE = 2.0**19
+
+
+def tile_parts(value):
+    high = value.astype(BF16)
+    return high, ((value - high.astype(F32)) * LOW_SCALE).astype(F8)
 
 
 ROW_SLOT, ROW_COL, ROW_KEEP, COL_SLOT, COL_ROW, COL_KEEP, ROW_LAST, COL_LAST, COL_HAS = range(9)
@@ -44,7 +52,7 @@
     depth, n_gx, n_gy, n_z,
     row_ref, col_ref, send_list, mass, moduli, guess, loads, tiles,
     sol, res,
-    stage, tile, tile_t, hist, rhs, ext, stress, scan, own, strain0, norm0, coef,
+    stage, tile, tile_low, tile_t, tile_t_low, hist, rhs, ext, stress, scan, own, strain0, norm0, coef,
     send_f, recv_f, send_r, recv_r, red_send, red_recv, table, tab, back_at, back_has,
     tile_sem, in_sem, tab_sem, fs_sem, fr_sem, rs_sem, rr_sem, ds_sem, dr_sem,
 ):
@@ -65,6 +73,7 @@
         (gx, (gy + n_gy - 1) % n_gy),
         (gx, (gy + 1) % n_gy),
     ]
+    there = [gx > 0, gx < n_gx - 1, gy > 0, gy < n_gy - 1]
     phases = [
         [(gx, (gy + k) % n_gy) for k in range(1, n_gy)],
         [(chip((y + k) % n_y, z), gy) for k in range(1, n_y)],
@@ -146,9 +155,17 @@
             device_id_type=MESH,
         )
 
+    def start(make, g):
+        for d in range(4):
+            pl.when(there[d])(make(g, d).start)
+
+    def wait_send(make, g):
+        for d in range(4):
+            pl.when(there[d])(make(g, d).wait_send)
+
     def wait_recv(make, g):
         for d in range(4):
-            make(g, d ^ 1).wait_recv()
+            pl.when(there[d])(make(g, d ^ 1).wait_recv)
 
     def pack(step, g):
         for d in range(4):
@@ -169,22 +186,23 @@
                 ext[g, blocks + d * depth + h, :rows] = high
                 ext[g, blocks + d * depth + h, rows:] = low
 
-    def sweep(source, g, weights, slot_at, block_at, keep_at):
+    def sweep(source, g, high, low, slot_at, block_at, keep_at):
         def body(i, total):
             for u in range(UNROLL):
                 t = i * UNROLL + u
                 x = source[g, tab[block_at, t]]
-                both = jnp.dot(
-                    jnp.concatenate([x, x], axis=1), weights[tab[slot_at, t]], preferred_element_type=F32
-                )
-                total = total * flag(keep_at, t) + (both[:rows] + both[rows:])
+                slot = tab[slot_at, t]
+                both = jnp.dot(x, high[slot], preferred_element_type=F32)
+                rest = jnp.dot(x[:rows], low[slot], preferred_element_type=F32)
+                both = both[:rows] + both[rows:] + rest * (1.0 / LOW_SCALE)
+                total = total * flag(keep_at, t) + both
                 scan[t] = total
             return total
 
         lax.fori_loop(0, slots // UNROLL, body, jnp.zeros((rows, block), F32))
 
     def strain_pass(step, g):
-        sweep(ext, g, tile_t, ROW_SLOT, ROW_COL, ROW_KEEP)
+        sweep(ext, g, tile_t, tile_t_low, ROW_SLOT, ROW_COL, ROW_KEEP)
         square = jnp.zeros((rows, block), F32)
         energy = jnp.zeros((rows, block), F32)
         if step == 2:
@@ -212,16 +230,14 @@
         return square, energy
 
     def back_pass(step, g):
-        sweep(stress, g, tile, COL_SLOT, COL_ROW, COL_KEEP)
+        sweep(stress, g, tile, tile_low, COL_SLOT, COL_ROW, COL_KEEP)
         if step > 0:
-            for d in range(4):
-                backward(g, d).wait_send()
+            wait_send(backward, g)
         for d in range(4):
             for h in range(depth):
                 e = blocks + d * depth + h
                 send_r[g, d, h] = scan[tab[COL_LAST, e]] * flag(COL_HAS, e)
-        for d in range(4):
-            backward(g, d).start()
+        start(backward, g)
         for b in range(blocks):
             own[g, b] = scan[tab[COL_LAST, b]] * flag(COL_HAS, b) + lanes(mass, b) * hist[step, g, b]
 
@@ -283,10 +299,17 @@
             piece(guess, hist.at[0], g, b, 0).wait()
     for g in groups:
         pack(0, g)
+    for d in range(4):
+
+        @pl.when(jnp.logical_not(there[d]))
+        def _():
+            for g in groups:
+                recv_f[g, d] = jnp.zeros_like(recv_f[g, d])
+                recv_r[g][d] = jnp.zeros_like(recv_r[g][d])
+
     pl.semaphore_wait(barrier, len(greet))
     for g in groups:
-        for d in range(4):
-            forward(g, d).start()
+        start(forward, g)
         split_own(0, g)
     to_smem = pltpu.make_async_copy(table, tab, tab_sem)
     to_smem.start()
@@ -297,12 +320,8 @@
         def split_tile(i, carry):
             t = c * per + i
             value = stage[t]
-            high, low = halves(value)
-            tile[t, :block] = high
-            tile[t, block:] = low
-            high, low = halves(value.T)
-            tile_t[t, :block] = high
-            tile_t[t, block:] = low
+            tile[t], tile_low[t] = tile_parts(value)
+            tile_t[t], tile_t_low[t] = tile_parts(value.T)
             return carry
 
         lax.fori_loop(0, per, split_tile, 0)
@@ -321,11 +340,9 @@
             if step == 0:
                 value = rhs[g, b] - value
             hist[step + 1, g, b] = value
-        for d in range(4):
-            forward(g, d).wait_send()
+        wait_send(forward, g)
         pack(step + 1, g)
-        for d in range(4):
-            forward(g, d).start()
+        start(forward, g)
         split_own(step + 1, g)
 
     def last(g):
@@ -348,36 +365,27 @@
         for b in range(blocks):
             piece(loads, rhs, g, b, 1).wait()
 
-    strain_half(0, 0)
-    back_pass(0, 0)
-    strain_half(0, 1)
-    finish(0, 0)
-    back_pass(0, 1)
-    strain_half(1, 0)
-    finish(0, 1)
-    back_pass(1, 0)
-    reduce_next(0, 0, 0)
-    strain_half(1, 1)
-    finish(1, 0)
-    reduce_next(0, 0, 1)
-    back_pass(1, 1)
-    reduce_next(0, 1, 0)
-    strain_half(2, 0)
-    finish(1, 1)
-    reduce_next(0, 1, 1)
-    back_pass(2, 0)
-    reduce_next(1, 0, 0)
-    strain_half(2, 1)
-    reduce_next(1, 0, 1)
-    back_pass(2, 1)
-    reduce_next(1, 1, 0)
+    turns = [(step, g) for step in range(3) for g in groups]
+    for q, (step, g) in enumerate(turns):
+        strain_half(step, g)
+        if q >= LAG and turns[q - LAG][0] < 2:
+            finish(*turns[q - LAG])
+        for ago, phase in ((2, 1), (1, 0)) if GROUPS > 2 else ((1, 1),):
+            if q >= ago and turns[q - ago][0] > 0:
+                reduce_next(turns[q - ago][0] - 1, turns[q - ago][1], phase)
+        back_pass(step, g)
+        if GROUPS == 2 and step > 0:
+            reduce_next(step - 1, g, 0)
+    if GROUPS > 2:
+        reduce_next(1, GROUPS - 1, 0)
+        reduce_next(1, GROUPS - 2, 1)
     last(0)
-    reduce_next(1, 1, 1)
-    last(1)
-    for g in groups:
-        for d in range(4):
-            forward(g, d).wait_send()
-            backward(g, d).wait_send()
+    reduce_next(1, GROUPS - 1, 1)
+    for g in groups[1:]:
+        last(g)
+    for g in groups:
+        wait_send(forward, g)
+        wait_send(backward, g)
         for which in range(2):
             for phase in range(3):
                 for copy in reduce_copies(which, g, phase):
@@ -408,8 +416,10 @@
             out_specs=[vmem, vmem],
             scratch_shapes=[
                 pltpu.VMEM((slots, block, block), F32),
-                pltpu.VMEM((slots, 2 * block, block), BF16),
-                pltpu.VMEM((slots, 2 * block, block), BF16),
+                pltpu.VMEM((slots, block, block), BF16),
+                pltpu.VMEM((slots, block, block), F8),
+                pltpu.VMEM((slots, block, block), BF16),
+                pltpu.VMEM((slots, block, block), F8),
                 pltpu.VMEM((3, GROUPS, blocks, rows, block), F32),
                 pltpu.VMEM((GROUPS, blocks, rows, block), F32),
                 pltpu.VMEM((GROUPS, extent, 2 * rows, block), BF16),

time: 75.8 us -> 69.1 us (0.912)
  Pallas kernels: 73.6 us -> 66.2 us
    pallas_call x1, Pallas kernels: 73.6 us -> 66.2 us  [on_device(): pl.pallas_call(functools.partial(solve_kernel, depth, n_gx, n_gy, n_z), o...]
where the time goes in v2:
time: 69.1 us; the launch traced here: 68.4 us
  Pallas kernels  66.2 us (96%)
  local copies, waits for them, and re-layouts  1.49 us (2%)
    pallas_call x1, Pallas kernels, on_device(): pl.pallas_call(functools.partial(solve_kernel, depth, n_gx, n_gy, n_z), o...  66.2 us
    unnamed x2, local copies, waits for them, and re-layouts  1.49 us

profile of v2, /device:TPU:32, one launch (start us, length us, event | category | flops | bytes accessed | tf_op | source)
XLA Modules:
  0.0 68.4 jit_solution(14241749017851649566)
XLA Ops:
  0.6 66.2 %solve.1 = (f32[64,1536]{1,0:T(8,128)S(1)}, f32[64,1536]{1,0:T(8,128)S(1)}) custom-call(s32[40]{0:T(128)} %row_ref.1, s32[40]{0:T(128)} %col_ref.1, s32[1,4,4]{2,1,0:T(4,128)} %send_list.1, f32[1536]{0:T(1024)} %mass.1, f32[1536]{0:T(1024)} %moduli.1, f32[64,1536]{1,0:T(8,128)} %guess.1, f32[64,1536]{1,0:T(8,128)} %loads.1, f32[40,256,256]{2,1,0:T(8,128)} %tiles.1), custom_call_target="tpu_custom_call" | custom-call | tf_op jit(solution)/shard_map/solve/pallas_call | solution.py:412
  66.9 0.7 %copy.12 = f32[64,1536]{1,0:T(8,128)} copy(f32[64,1536]{1,0:T(8,128)S(1)} %get-tuple-element.2) | data formatting | bytes 786432
  67.6 0.7 %copy.13 = f32[64,1536]{1,0:T(8,128)} copy(f32[64,1536]{1,0:T(8,128)S(1)} %get-tuple-element.3) | data formatting | bytes 786432

commit v3 on v2

--- a/solution.py
+++ b/solution.py
@@ -10,8 +10,10 @@
 MESH = pl.DeviceIdType.MESH
 GROUPS = 4
 LAG = 2
+PIECES = 1
+EARLY = 3
 CHUNKS = 8
-UNROLL = 20
+UNROLL = 40
 F32 = jnp.float32
 BF16 = jnp.bfloat16
 F8 = jnp.float8_e4m3fn
@@ -60,6 +62,7 @@
     blocks, rows = hist.shape[2:4]
     extent = blocks + 4 * depth
     groups = range(GROUPS)
+    pieces = [(p, pl.ds(p * (rows // PIECES), rows // PIECES)) for p in range(PIECES)]
     gx, gy = lax.axis_index("gx"), lax.axis_index("gy")
     n_y = n_gx // n_z
     y, z = gx // n_z, gx % n_z
@@ -135,43 +138,43 @@
     def lanes(ref, b):
         return ref[b * block : (b + 1) * block].reshape(1, block)
 
-    def forward(g, d):
+    def forward(g, p, d):
         return pltpu.make_async_remote_copy(
-            src_ref=send_f.at[g, d],
-            dst_ref=recv_f.at[g, d ^ 1],
-            send_sem=fs_sem.at[g, d],
-            recv_sem=fr_sem.at[g, d ^ 1],
+            src_ref=send_f.at[g, p, d],
+            dst_ref=recv_f.at[g, p, d ^ 1],
+            send_sem=fs_sem.at[g, p, d],
+            recv_sem=fr_sem.at[g, p, d ^ 1],
             device_id=around[d],
             device_id_type=MESH,
         )
 
-    def backward(g, d):
+    def backward(g, p, d):
         return pltpu.make_async_remote_copy(
-            src_ref=send_r.at[g, d],
-            dst_ref=recv_r[g].at[d ^ 1],
-            send_sem=rs_sem.at[g, d],
-            recv_sem=rr_sem.at[g, d ^ 1],
+            src_ref=send_r.at[g, p, d],
+            dst_ref=recv_r[g][p].at[d ^ 1],
+            send_sem=rs_sem.at[g, p, d],
+            recv_sem=rr_sem.at[g, p, d ^ 1],
             device_id=around[d],
             device_id_type=MESH,
         )
 
-    def start(make, g):
-        for d in range(4):
-            pl.when(there[d])(make(g, d).start)
-
-    def wait_send(make, g):
-        for d in range(4):
-            pl.when(there[d])(make(g, d).wait_send)
-
-    def wait_recv(make, g):
-        for d in range(4):
-            pl.when(there[d])(make(g, d ^ 1).wait_recv)
-
-    def pack(step, g):
+    def start(make, g, p):
+        for d in range(4):
+            pl.when(there[d])(make(g, p, d).start)
+
+    def wait_send(make, g, p):
+        for d in range(4):
+            pl.when(there[d])(make(g, p, d).wait_send)
+
+    def wait_recv(make, g, p):
+        for d in range(4):
+            pl.when(there[d])(make(g, p, d ^ 1).wait_recv)
+
+    def pack(step, g, p, part):
         for d in range(4):
             for h in range(depth):
                 at, has = listed(d, h)
-                send_f[g, d, h] = hist[step, g, at] * has
+                send_f[g, p, d, h] = hist[step, g, at, part] * has
 
     def split_own(step, g):
         for b in range(blocks):
@@ -179,12 +182,12 @@
             ext[g, b, :rows] = high
             ext[g, b, rows:] = low
 
-    def split_halo(g):
+    def split_halo(g, p, part):
         for d in range(4):
             for h in range(depth):
-                high, low = halves(recv_f[g, d, h])
-                ext[g, blocks + d * depth + h, :rows] = high
-                ext[g, blocks + d * depth + h, rows:] = low
+                high, low = halves(recv_f[g, p, d, h])
+                ext[g, blocks + d * depth + h, part] = high
+                ext[g, blocks + d * depth + h, pl.ds(rows + part.start, part.size)] = low
 
     def sweep(source, g, high, low, slot_at, block_at, keep_at):
         def body(i, total):
@@ -231,21 +234,22 @@
 
     def back_pass(step, g):
         sweep(stress, g, tile, tile_low, COL_SLOT, COL_ROW, COL_KEEP)
-        if step > 0:
-            wait_send(backward, g)
-        for d in range(4):
-            for h in range(depth):
-                e = blocks + d * depth + h
-                send_r[g, d, h] = scan[tab[COL_LAST, e]] * flag(COL_HAS, e)
-        start(backward, g)
+        for p, part in pieces:
+            if step > 0:
+                wait_send(backward, g, p)
+            for d in range(4):
+                for h in range(depth):
+                    e = blocks + d * depth + h
+                    send_r[g, p, d, h] = scan[tab[COL_LAST, e], part] * flag(COL_HAS, e)
+            start(backward, g, p)
         for b in range(blocks):
             own[g, b] = scan[tab[COL_LAST, b]] * flag(COL_HAS, b) + lanes(mass, b) * hist[step, g, b]
 
-    def total_of(g, b):
-        total = own[g, b]
+    def total_of(g, b, p, part):
+        total = own[g, b, part]
         for d in range(4):
             k = d * blocks + b
-            total += recv_r[g][d, back_at[k]] * back_has[k].astype(F32)
+            total += recv_r[g][p][d, back_at[k]] * back_has[k].astype(F32)
         return total
 
     def reduce_copies(which, g, phase):
@@ -298,23 +302,18 @@
         for b in range(blocks):
             piece(guess, hist.at[0], g, b, 0).wait()
     for g in groups:
-        pack(0, g)
+        for p, part in pieces:
+            pack(0, g, p, part)
     for d in range(4):
 
         @pl.when(jnp.logical_not(there[d]))
         def _():
             for g in groups:
-                recv_f[g, d] = jnp.zeros_like(recv_f[g, d])
-                recv_r[g][d] = jnp.zeros_like(recv_r[g][d])
-
-    pl.semaphore_wait(barrier, len(greet))
-    for g in groups:
-        start(forward, g)
-        split_own(0, g)
-    to_smem = pltpu.make_async_copy(table, tab, tab_sem)
-    to_smem.start()
-
-    for c in range(CHUNKS):
+                for p in range(PIECES):
+                    recv_f[g, p, d] = jnp.zeros_like(recv_f[g, p, d])
+                    recv_r[g][p][d] = jnp.zeros_like(recv_r[g][p][d])
+
+    def split_chunk(c):
         loads_in[c].wait()
 
         def split_tile(i, carry):
@@ -326,27 +325,42 @@
 
         lax.fori_loop(0, per, split_tile, 0)
 
+    for c in range(EARLY):
+        split_chunk(c)
+    pl.semaphore_wait(barrier, len(greet))
+    for g in groups:
+        for p, _ in pieces:
+            start(forward, g, p)
+        split_own(0, g)
+    to_smem = pltpu.make_async_copy(table, tab, tab_sem)
+    to_smem.start()
+    for c in range(EARLY, CHUNKS):
+        split_chunk(c)
+
     def strain_half(step, g):
-        wait_recv(forward, g)
-        split_halo(g)
+        for p, part in pieces:
+            wait_recv(forward, g, p)
+            split_halo(g, p, part)
         square, energy = strain_pass(step, g)
         if step > 0:
             reduce_start(step - 1, g, square, energy)
 
     def finish(step, g):
-        wait_recv(backward, g)
-        for b in range(blocks):
-            value = total_of(g, b)
-            if step == 0:
-                value = rhs[g, b] - value
-            hist[step + 1, g, b] = value
-        wait_send(forward, g)
-        pack(step + 1, g)
-        start(forward, g)
+        for p, part in pieces:
+            wait_recv(backward, g, p)
+            for b in range(blocks):
+                value = total_of(g, b, p, part)
+                if step == 0:
+                    value = rhs[g, b, part] - value
+                hist[step + 1, g, b, part] = value
+            wait_send(forward, g, p)
+            pack(step + 1, g, p, part)
+            start(forward, g, p)
         split_own(step + 1, g)
 
     def last(g):
-        wait_recv(backward, g)
+        for p, _ in pieces:
+            wait_recv(backward, g, p)
         norm, curve = reduce_end(1, g)
         alpha0 = coef[g, 0]
         beta = norm / norm0[g]
@@ -354,11 +368,11 @@
         alpha0, alpha1, beta = wide(alpha0), wide(alpha1), wide(beta)
         for b in range(blocks):
             r0, w1 = hist[1, g, b], hist[2, g, b]
-            w2 = total_of(g, b)
+            w2 = jnp.concatenate([total_of(g, b, p, part) for p, part in pieces], axis=0)
             r1 = r0 - alpha0 * w1
-            part = (slice(g * rows, (g + 1) * rows), slice(b * block, (b + 1) * block))
-            sol[part] = hist[0, g, b] + alpha0 * r0 + alpha1 * (r1 + beta * r0)
-            res[part] = r1 - alpha1 * (w1 - alpha0 * w2 + beta * w1)
+            place = (slice(g * rows, (g + 1) * rows), slice(b * block, (b + 1) * block))
+            sol[place] = hist[0, g, b] + alpha0 * r0 + alpha1 * (r1 + beta * r0)
+            res[place] = r1 - alpha1 * (w1 - alpha0 * w2 + beta * w1)
 
     to_smem.wait()
     for g in groups:
@@ -384,8 +398,9 @@
     for g in groups[1:]:
         last(g)
     for g in groups:
-        wait_send(forward, g)
-        wait_send(backward, g)
+        for p, _ in pieces:
+            wait_send(forward, g, p)
+            wait_send(backward, g, p)
         for which in range(2):
             for phase in range(3):
                 for copy in reduce_copies(which, g, phase):
@@ -407,7 +422,7 @@
         vmem = pl.BlockSpec(memory_space=pltpu.VMEM)
         hbm = pl.BlockSpec(memory_space=pl.ANY)
         peers = (n_gy - 1) + (n_gx // n_z - 1) + (n_z - 1)
-        halo = (GROUPS, 4, depth, rows, block)
+        halo = (GROUPS, PIECES, 4, depth, rows // PIECES, block)
         dma = pltpu.SemaphoreType.DMA
         return pl.pallas_call(
             functools.partial(solve_kernel, depth, n_gx, n_gy, n_z),
@@ -432,7 +447,7 @@
                 pltpu.VMEM(halo, F32),
                 pltpu.VMEM(halo, F32),
                 pltpu.VMEM(halo, F32),
-                [pltpu.VMEM(halo[1:], F32)] * GROUPS,
+                [[pltpu.VMEM(halo[2:], F32)] * PIECES] * GROUPS,
                 pltpu.VMEM((2, GROUPS, 3, 1, 128), F32),
                 pltpu.VMEM((2, GROUPS, peers, 1, 128), F32),
                 pltpu.VMEM((16, 128), jnp.int32),
@@ -442,10 +457,10 @@
                 dma((CHUNKS,)),
                 dma((2, GROUPS, blocks)),
                 dma,
-                dma((GROUPS, 4)),
-                dma((GROUPS, 4)),
-                dma((GROUPS, 4)),
-                dma((GROUPS, 4)),
+                dma((GROUPS, PIECES, 4)),
+                dma((GROUPS, PIECES, 4)),
+                dma((GROUPS, PIECES, 4)),
+                dma((GROUPS, PIECES, 4)),
                 dma((2, GROUPS, peers)),
                 dma((2, GROUPS, peers)),
             ],

time: 69.1 us -> 68.7 us (level)
  no operation moved by 1% of the time
where the time goes in v3:
time: 68.7 us; the launch traced here: 68.6 us
  Pallas kernels  66.5 us (97%)
  local copies, waits for them, and re-layouts  1.49 us (2%)
    pallas_call x1, Pallas kernels, on_device(): pl.pallas_call(functools.partial(solve_kernel, depth, n_gx, n_gy, n_z), o...  66.5 us
    unnamed x2, local copies, waits for them, and re-layouts  1.49 us

profile of v3, /device:TPU:32, one launch (start us, length us, event | category | flops | bytes accessed | tf_op | source)
XLA Modules:
  0.0 68.6 jit_solution(13623642511609945901)
XLA Ops:
  0.6 66.5 %solve.1 = (f32[64,1536]{1,0:T(8,128)S(1)}, f32[64,1536]{1,0:T(8,128)S(1)}) custom-call(s32[40]{0:T(128)} %row_ref.1, s32[40]{0:T(128)} %col_ref.1, s32[1,4,4]{2,1,0:T(4,128)} %send_list.1, f32[1536]{0:T(1024)} %mass.1, f32[1536]{0:T(1024)} %moduli.1, f32[64,1536]{1,0:T(8,128)} %guess.1, f32[64,1536]{1,0:T(8,128)} %loads.1, f32[40,256,256]{2,1,0:T(8,128)} %tiles.1), custom_call_target="tpu_custom_call" | custom-call | tf_op jit(solution)/shard_map/solve/pallas_call | solution.py:427
  67.1 0.7 %copy.12 = f32[64,1536]{1,0:T(8,128)} copy(f32[64,1536]{1,0:T(8,128)S(1)} %get-tuple-element.2) | data formatting | bytes 786432
  67.9 0.7 %copy.13 = f32[64,1536]{1,0:T(8,128)} copy(f32[64,1536]{1,0:T(8,128)S(1)} %get-tuple-element.3) | data formatting | bytes 786432
